TPU v7x, 32 devices: a whole 2x2x4 slice. The times are simulated.
32 devices in a mesh: dev: 32 (over z, y, x, core).
Axes of the slice: x: 2, y: 2, z: 4, core: 2. Of those that a mesh axis runs over, the one named last changes fastest.
Arguments:
- dual_blocks: bfloat16 [32, 3072, 3072], P('dev'), as said below
- rigid_modes: float32 [32, 6, 3072], P('dev'), may hold values from -5 to 5
- dual_local: float32 [32, 8, 3072], P('dev'), may hold values from -6 to 6
- coarse_rhs: float32 [32, 6, 8], P('dev'), may hold values from -4608 to 4608
- iface_sizes: int32 [32], P('dev'), may hold values from 1536 to 3072, as said below
- neighbours: int32 [32, 6], P('dev'), may hold values from -1 to 31, as said below
- shared_counts: int32 [32, 6], P('dev'), may hold values from 256 to 512, as said below
- iface_map: int32 [32, 3072], P('dev'), may hold values from -1 to 3071, as said below
- owner: int32 [32], replicated, may hold values from 0 to 31, as said below
Outputs:
- multipliers: float32 [32, 8, 3072], P('dev')
- projected_residual: float32 [32, 8, 3072], P('dev')
Inputs may be any that keep to these rules, and one draw needn't show every extreme that they name: `dual_blocks`: each block is symmetric positive definite, and so is each of its leading principal parts. Grid subdomain g is held by slot owner[g] = (g + s) mod 32 for one offset s of the draw, so the subdomains across the faces -x, +x, -y, +y, -z, +z of slot i sit in slots i - 1, i + 1, i - 4, i + 4, i - 16, i + 16, taken mod 32. `neighbours`: the subdomains form a grid of 4 x 4 x 32/16 with g = x + 4 y + 16 z. Row i lists, for the faces -x, +x, -y, +y, -z, +z of the subdomain held in slot i, the grid subdomain across that face, or -1 on the outer boundary; across a face from g the opposite face names g. `shared_counts`: equal on both sides of a shared face; some subdomain has 512 on all its faces. `iface_sizes`: the sum of the slot's shared_counts row; some subdomain has 3072. `iface_map`: for j < iface_sizes[i], entry j is f * 512 + p for the dof at position p of face f of slot i (p below that face's count), each such code once; -1 beyond. The dof at position p of a shared face pairs with the dof at position p of the opposite face of the neighbour.
All inputs are finite; a program needn't handle non-finite values.
Results may differ from a plain program's by a relative error of at most 0.025.
Values sent between devices are 32-bit elements; how exact they have to be, the bound alone decides.
A program may use at most 128 MiB of HBM per device.

v0:
```python
import jax
import jax.numpy as jnp
from jax import lax
from jax.sharding import PartitionSpec as P

FACES = 6
MODES = 6
CAP = 512
NMAX = 3072
ITERS = 3
HIGHEST_PRECISION = lax.Precision.HIGHEST
OPPOSITE = (1, 0, 3, 2, 5, 4)
FACE_STEPS = (-1, 1, -4, 4, -16, 16)


def from_behind(value, axis, by):
    length = lax.axis_size(axis)
    return lax.ppermute(value, axis, [(i, (i + by) % length) for i in range(length)])


def solve_coarse(factor, vector):
    middle = lax.linalg.triangular_solve(factor, vector, left_side=True, lower=True)
    return lax.linalg.triangular_solve(factor, middle, left_side=True, lower=True, transpose_a=True)


def per_device(
    dual_blocks,
    rigid_modes,
    dual_local,
    coarse_rhs,
    iface_sizes,
    neighbours,
    shared_counts,
    iface_map,
    owner,
):
    my_slot = lax.axis_index("dev")
    devices = lax.axis_size("dev")
    loads = dual_local.shape[1]
    columns = jnp.arange(NMAX, dtype=jnp.int32)
    live_dofs = columns < iface_sizes[0]
    dof_codes = jnp.clip(jnp.where(live_dofs, iface_map[0], 0), 0, FACES * CAP - 1)
    which_face = dof_codes // CAP
    position = dof_codes % CAP
    face_row = neighbours[0]
    count_row = shared_counts[0]
    face_onehot = which_face[None, :] == jnp.arange(FACES, dtype=jnp.int32)[:, None]
    has_partner = jnp.any(face_onehot & (face_row >= 0)[:, None], axis=0)
    face_limit = jnp.sum(jnp.where(face_onehot, count_row[:, None], 0), axis=0)
    shared = live_dofs & has_partner & (position < face_limit)
    live_float = live_dofs.astype(jnp.float32)
    shared_float = shared.astype(jnp.float32)
    weights = jnp.where(shared, 0.5, live_float)
    targets = jnp.where(live_dofs, dof_codes, FACES * CAP)
    inverse = (
        jnp.full((FACES * CAP,), NMAX, jnp.int32)
        .at[targets]
        .set(columns, mode="drop")
        .reshape(FACES, CAP)
    )
    partner_slot = jnp.where(face_row >= 0, owner[jnp.clip(face_row, 0, owner.shape[0] - 1)], 0)
    face_mask = (
        (face_row >= 0)[:, None] & (jnp.arange(CAP, dtype=jnp.int32)[None, :] < count_row[:, None])
    ).astype(jnp.float32)

    def gather_faces(values):
        padded = jnp.concatenate([values, jnp.zeros((values.shape[0], 1), values.dtype)], axis=1)
        return jnp.take(padded, inverse, axis=1)

    def across_faces(face_vals, mover):
        pieces = [mover(face_vals[:, OPPOSITE[face]], -FACE_STEPS[face]) for face in range(FACES)]
        return jnp.stack(pieces, axis=1) * face_mask[None]

    def spread_back(far_faces):
        flattened = far_faces.reshape(far_faces.shape[0], FACES * CAP)
        return jnp.take(flattened, dof_codes, axis=1) * shared_float[None]

    def combine(values, far_faces):
        return live_float[None] * (values - spread_back(far_faces))

    def partial_inner(left_vec, right_vec):
        return jnp.sum(weights[None] * left_vec * right_vec, axis=1)

    modes_live = rigid_modes[0] * live_float[None]
    local_rhs = dual_local[0]
    own_modes = gather_faces(modes_live)
    own_rhs = gather_faces(local_rhs)
    setup_pieces = [
        from_behind(
            (own_modes[:, OPPOSITE[face]], own_rhs[:, OPPOSITE[face]]), "dev", -FACE_STEPS[face]
        )
        for face in range(FACES)
    ]
    far_modes = jnp.stack([piece[0] for piece in setup_pieces], axis=1) * face_mask[None]
    far_rhs = jnp.stack([piece[1] for piece in setup_pieces], axis=1) * face_mask[None]
    dual_rhs = combine(local_rhs, far_rhs)
    diagonal = lax.dot_general(
        modes_live, modes_live, (((1,), (1,)), ((), ())), precision=HIGHEST_PRECISION
    )
    coupling = -jnp.einsum("afp,bfp->afb", own_modes, far_modes, precision=HIGHEST_PRECISION)
    block_row = jnp.zeros((MODES, devices, MODES), jnp.float32).at[:, my_slot, :].set(diagonal)
    block_row = block_row.at[:, partner_slot, :].add(coupling)
    coarse_matrix, coarse_goal = (
        lax.all_gather(block_row.reshape(MODES, devices * MODES), "dev", axis=0, tiled=True),
        lax.all_gather(coarse_rhs[0], "dev", axis=0, tiled=True),
    )
    factor = jnp.linalg.cholesky(coarse_matrix)

    def modes_apply(solution):
        stacked = solution.reshape(devices, MODES, loads)
        own_part = lax.dot_general(
            stacked[my_slot], modes_live, (((0,), (0,)), ((), ())), precision=HIGHEST_PRECISION
        )
        far_part = jnp.einsum(
            "bfp,fbl->lfp", far_modes, stacked[partner_slot], precision=HIGHEST_PRECISION
        )
        return combine(own_part, far_part)

    def project(residual):
        coarse_part = lax.dot_general(
            modes_live, residual, (((1,), (1,)), ((), ())), precision=HIGHEST_PRECISION
        )
        placed = jnp.zeros((devices, MODES, loads), jnp.float32).at[my_slot].set(coarse_part)
        coarse_all = lax.psum(placed, "dev").reshape(devices * MODES, loads)
        solution = solve_coarse(factor, coarse_all)
        projected = residual - modes_apply(solution)
        norm_sq = lax.psum(partial_inner(projected, projected), "dev")
        return (projected, norm_sq)

    def dual_apply(vector):
        products = lax.dot_general(
            vector.astype(jnp.bfloat16),
            dual_blocks[0],
            (((1,), (1,)), ((), ())),
            preferred_element_type=jnp.float32,
        )
        far_part = across_faces(
            gather_faces(products), lambda piece, offset: from_behind(piece, "dev", offset)
        )
        return combine(products, far_part)

    multipliers = modes_apply(solve_coarse(factor, coarse_goal))
    residual = dual_rhs - dual_apply(multipliers)
    projected, norm_sq = project(residual)
    direction = projected
    for step_index in range(ITERS):
        applied = dual_apply(direction)
        curvature = lax.psum(partial_inner(direction, applied), "dev")
        step_size = norm_sq / curvature
        multipliers = multipliers + step_size[:, None] * direction
        residual = residual - step_size[:, None] * applied
        projected, norm_next = project(residual)
        direction = projected + (norm_next / norm_sq)[:, None] * direction
        norm_sq = norm_next
    return (multipliers[None], projected[None])


def solution(mesh):
    return jax.shard_map(
        per_device,
        mesh=mesh,
        in_specs=(
            P("dev", None, None),
            P("dev", None, None),
            P("dev", None, None),
            P("dev", None, None),
            P("dev"),
            P("dev", None),
            P("dev", None),
            P("dev", None),
            P(),
        ),
        out_specs=(P("dev", None, None), P("dev", None, None)),
        check_vma=False,
    )
```

profile of v0, /device:TPU:0, one launch (start us, length us, event | category | flops | bytes accessed | tf_op | source)
XLA Modules:
  0.0 945.2 jit_solution(9198826558787820039)
XLA Ops:
  2.1 11.8 %scatter_custom_fusion = s32[3072]{0:T(1024)S(1)} fusion(s32[3072]{0:T(1024)S(1)} %bitcast.527, s32[3072]{0:T(1024)S(1)} %iota.115, s32[]{:T(128)} %constant.261.clone.1), kind=kCustom, calls=%fused_computation.314 | custom fusion | bytes 12292 | tf_op jit(solution)/shard_map/scatter | solution.py:58
  16.0 10.9 %gather_fusion.1 = f32[3072,6]{1,0:T(8,128)} fusion(f32[6,3073]{0,1:T(8,128)S(1)} %concatenate.51, s32[3072]{0:T(1024)S(1)} %broadcast_clamp_fusion.1), kind=kCustom, calls=%fused_computation.16 | custom fusion | bytes 159744 | tf_op jit(solution)/shard_map/jit(_take)/gather | solution.py:68
  26.9 1.9 copy.135
  30.0 5.9 collective-permute-start.1
  36.0 4.7 collective-permute-start.3
  47.6 36.6 %all-gather = f32[1,192,8]{2,0,1:T(1,128)S(1)} all-gather(f32[1,6,8]{2,0,1:T(1,128)S(1)} %copy-done.67), channel_id=2, replica_groups=mesh['dev'=32] {'dev'}, dimensions={1}, use_global_device_ids=true | all-gather | bytes 6336 | tf_op jit(solution)/shard_map/all_gather | solution.py:105
  86.1 9.5 %gather_fusion.8 = f32[3072,8]{1,0:T(8,128)S(1)} fusion(f32[8,3073]{0,1:T(8,128)} %concatenate.52.clone, s32[3072]{0:T(1024)S(1)} %get-tuple-element.217), kind=kCustom, calls=%fused_computation.1.clone | custom fusion | bytes 208896 | tf_op jit(solution)/shard_map/jit(_take)/gather | solution.py:68
  101.8 2.0 scatter_fusion
  104.8 39.5 %all-gather.1 = f32[32,6,192]{2,1,0:T(8,128)S(1)} all-gather(f32[1,6,192]{2,1,0:T(8,128)S(1)} %reshape.887), channel_id=1, replica_groups=mesh['dev'=32] {'dev'}, dimensions={0}, use_global_device_ids=true | all-gather | bytes 152064 | tf_op jit(solution)/shard_map/all_gather | solution.py:104
  144.5 11.7 %cholesky.51 = f32[128,128]{1,0:T(8,128)S(1)} custom-call(f32[128,128]{1,0:T(8,128)S(1)} %cholesky.124), custom_call_target="Cholesky" | custom-call | tf_op jit(solution)/shard_map/jit(cholesky)/cholesky | solution.py:107
  156.2 9.8 %custom-call.17 = f32[1,128,128]{1,2,0:T(8,128)S(1)} custom-call(f32[1,128,128]{2,1,0:T(8,128)S(1)} %get-tuple-element.201), custom_call_target="InvertDiagBlocksLowerTriangular" | custom-call | tf_op jit(solution)/shard_map/jit(cholesky)/cholesky | solution.py:107
  166.4 5.8 cholesky.110
  175.0 19.8 %custom-call.27 = f32[2,128,128]{1,2,0:T(8,128)S(1)} custom-call(f32[2,128,128]{2,1,0:T(8,128)S(1)} %pad_maximum_fusion), custom_call_target="InvertDiagBlocksLowerTriangular" | custom-call | tf_op jit(solution)/shard_map/triangular_solve/custom-call.4 | solution.py:23
  199.3 10.9 %gather_fusion.7 = f32[3072,8]{1,0:T(8,128)} fusion(f32[8,3072]{0,1:T(8,128)S(1)} %copy.143, s32[3072]{0:T(1024)S(1)} %get-tuple-element.216), kind=kCustom, calls=%fused_computation.clone | custom fusion | bytes 208896 | tf_op jit(solution)/shard_map/jit(_take)/gather | solution.py:76
  212.9 12.0 %fusion.6 = f32[8,3072]{1,0:T(8,128)} fusion(bf16[1,3072,3072]{2,1,0:T(8,128)(2,1)} %param.27, f32[8,3072]{1,0:T(8,128)S(1)} %fusion.17), kind=kOutput, calls=%fused_computation.30 | convolution fusion | flops 151019520 | bytes 19070976 | tf_op jit(solution)/shard_map/dot_general | solution.py:131
  227.6 9.5 %gather_fusion.10 = f32[3072,8]{1,0:T(8,128)S(1)} fusion(f32[8,3073]{0,1:T(8,128)} %concatenate.53.clone, s32[3072]{0:T(1024)S(1)} %get-tuple-element.217), kind=kCustom, calls=%fused_computation.11.clone | custom fusion | bytes 208896 | tf_op jit(solution)/shard_map/jit(_take)/gather | solution.py:68
  239.6 5.0 collective-permute-start.7
  244.6 4.7 collective-permute-start.9
  249.4 6.7 collective-permute-done.12
  258.0 4.7 collective-permute-start.15
  262.7 2.9 collective-permute-start.17
  270.8 2.5 copy.151
  273.3 3.7 bitcast_multiply_fusion.4
  277.0 12.6 %gather_fusion.11 = f32[3072,8]{1,0:T(8,128)} fusion(f32[8,3072]{0,1:T(8,128)} %get-tuple-element.205, s32[3072]{0:T(1024)S(1)} %get-tuple-element.216), kind=kCustom, calls=%fused_computation.3.clone | custom fusion | bytes 208896 | tf_op jit(solution)/shard_map/jit(_take)/gather | solution.py:76
  289.6 2.5 copy.152
  292.1 10.9 %gather_fusion.9 = f32[3072,8]{1,0:T(8,128)} fusion(f32[8,3072]{0,1:T(8,128)S(1)} %copy-done.2, s32[3072]{0:T(1024)S(1)} %get-tuple-element.216), kind=kCustom, calls=%fused_computation.2.clone | custom fusion | bytes 208896 | tf_op jit(solution)/shard_map/jit(_take)/gather | solution.py:76
  305.6 3.3 fusion.19
  309.1 37.8 %psum.70 = f32[192,8]{0,1:T(8,128)S(1)} all-reduce(f32[192,8]{0,1:T(8,128)S(1)} %reshape.519), channel_id=1, replica_groups=mesh['dev'=32] {'dev'}, use_global_device_ids=true, to_apply=%region_10.15 | all-reduce | flops 1536 | bytes 12288 | tf_op jit(solution)/shard_map/psum | solution.py:124
  353.6 10.9 %gather_fusion.12 = f32[3072,8]{1,0:T(8,128)} fusion(f32[8,3072]{0,1:T(8,128)S(1)} %copy.157, s32[3072]{0:T(1024)S(1)} %get-tuple-element.216), kind=kCustom, calls=%fused_computation.4.clone | custom fusion | bytes 208896 | tf_op jit(solution)/shard_map/jit(_take)/gather | solution.py:76
  366.6 12.0 %fusion.4 = f32[8,3072]{1,0:T(8,128)} fusion(bf16[1,3072,3072]{2,1,0:T(8,128)(2,1)} %param.27, f32[8,3072]{1,0:T(8,128)S(1)} %fusion.16), kind=kOutput, calls=%fused_computation.28 | convolution fusion | flops 151019520 | bytes 19070976 | tf_op jit(solution)/shard_map/dot_general | solution.py:131
  381.3 11.0 %gather_fusion.13 = f32[3072,8]{1,0:T(8,128)S(1)} fusion(f32[8,3073]{0,1:T(8,128)} %concatenate.55.clone, s32[3072]{0:T(1024)} %copy-done.45), kind=kCustom, calls=%fused_computation.12.clone | custom fusion | bytes 208896 | tf_op jit(solution)/shard_map/jit(_take)/gather | solution.py:68
  394.4 5.3 collective-permute-start.19
  399.7 4.7 collective-permute-start.21
  404.4 2.9 collective-permute-start.23
  412.3 2.4 bitcast_multiply_fusion.2
  414.7 13.8 %gather_fusion.14 = f32[3072,8]{1,0:T(8,128)} fusion(f32[8,3072]{0,1:T(8,128)} %bitcast_multiply_fusion.2, s32[3072]{0:T(1024)} %copy-done.34), kind=kCustom, calls=%fused_computation.5.clone | custom fusion | bytes 208896 | tf_op jit(solution)/shard_map/jit(_take)/gather | solution.py:76
  430.6 38.5 %all-reduce.11 = (f32[8]{0:T(128)S(1)}, f32[8]{0:T(128)S(1)}) all-reduce(f32[8]{0:T(128)S(1)} %get-tuple-element.155, f32[8]{0:T(128)S(1)} %get-tuple-element.154), channel_id=1, replica_groups=mesh['dev'=32] {'dev'}, use_global_device_ids=true, to_apply=%region_12.17 | all-reduce | flops 16 | bytes 128 | tf_op jit(solution)/shard_map/psum | solution.py:127
  469.8 3.3 fusion.20
  473.3 39.3 %psum.73 = f32[192,8]{0,1:T(8,128)S(1)} all-reduce(f32[192,8]{0,1:T(8,128)S(1)} %reshape.523), channel_id=1, replica_groups=mesh['dev'=32] {'dev'}, use_global_device_ids=true, to_apply=%region_15.20 | all-reduce | flops 1536 | bytes 12288 | tf_op jit(solution)/shard_map/psum | solution.py:124
  518.6 10.9 %gather_fusion.15 = f32[3072,8]{1,0:T(8,128)} fusion(f32[8,3072]{0,1:T(8,128)S(1)} %copy.167, s32[3072]{0:T(1024)S(1)} %copy-done.35), kind=kCustom, calls=%fused_computation.6.clone | custom fusion | bytes 208896 | tf_op jit(solution)/shard_map/jit(_take)/gather | solution.py:76
  531.8 40.7 %psum.74 = f32[8]{0:T(128)S(1)} all-reduce(f32[8]{0:T(128)S(1)} %get-tuple-element.210), channel_id=1, replica_groups=mesh['dev'=32] {'dev'}, use_global_device_ids=true, to_apply=%region_17.22 | all-reduce | flops 8 | bytes 64 | tf_op jit(solution)/shard_map/psum | solution.py:127
  573.2 12.0 %fusion.2 = f32[8,3072]{1,0:T(8,128)} fusion(bf16[1,3072,3072]{2,1,0:T(8,128)(2,1)} %param.27, f32[8,3072]{1,0:T(8,128)S(1)} %multiply_add_fusion.1), kind=kOutput, calls=%fused_computation.26 | convolution fusion | flops 151019520 | bytes 19070976 | tf_op jit(solution)/shard_map/dot_general | solution.py:131
  587.8 11.0 %gather_fusion.16 = f32[3072,8]{1,0:T(8,128)S(1)} fusion(f32[8,3073]{0,1:T(8,128)} %concatenate.56.clone, s32[3072]{0:T(1024)} %copy-done.45), kind=kCustom, calls=%fused_computation.13.clone | custom fusion | bytes 208896 | tf_op jit(solution)/shard_map/jit(_take)/gather | solution.py:68
  600.9 5.3 collective-permute-start.25
  606.2 4.9 collective-permute-start.27
  611.1 2.9 collective-permute-start.29
  619.0 2.4 bitcast_multiply_fusion.1
  621.4 13.4 %gather_fusion.17 = f32[3072,8]{1,0:T(8,128)} fusion(f32[8,3072]{0,1:T(8,128)} %bitcast_multiply_fusion.1, s32[3072]{0:T(1024)} %copy-done.34), kind=kCustom, calls=%fused_computation.7.clone | custom fusion | bytes 208896 | tf_op jit(solution)/shard_map/jit(_take)/gather | solution.py:76
  636.8 38.5 %psum.75 = f32[8]{0:T(128)S(1)} all-reduce(f32[8]{0:T(128)S(1)} %multiply_reduce_fusion.1), channel_id=1, replica_groups=mesh['dev'=32] {'dev'}, use_global_device_ids=true, to_apply=%region_19.24 | all-reduce | flops 8 | bytes 64 | tf_op jit(solution)/shard_map/psum | solution.py:148
  676.1 3.3 fusion.21
  679.7 39.3 %psum.76 = f32[192,8]{0,1:T(8,128)S(1)} all-reduce(f32[192,8]{0,1:T(8,128)S(1)} %reshape.527), channel_id=1, replica_groups=mesh['dev'=32] {'dev'}, use_global_device_ids=true, to_apply=%region_20.25 | all-reduce | flops 1536 | bytes 12288 | tf_op jit(solution)/shard_map/psum | solution.py:124
  725.5 11.9 %gather_fusion.18 = f32[3072,8]{1,0:T(8,128)} fusion(f32[8,3072]{0,1:T(8,128)S(1)} %copy.177, s32[3072]{0:T(1024)} %copy-done.34), kind=kCustom, calls=%fused_computation.8.clone | custom fusion | bytes 208896 | tf_op jit(solution)/shard_map/jit(_take)/gather | solution.py:76
  739.8 40.8 %psum.77 = f32[8]{0:T(128)S(1)} all-reduce(f32[8]{0:T(128)S(1)} %get-tuple-element.212), channel_id=1, replica_groups=mesh['dev'=32] {'dev'}, use_global_device_ids=true, to_apply=%region_22.27 | all-reduce | flops 8 | bytes 64 | tf_op jit(solution)/shard_map/psum | solution.py:127
  781.1 12.0 %fusion = f32[8,3072]{1,0:T(8,128)} fusion(bf16[1,3072,3072]{2,1,0:T(8,128)(2,1)} %param.27, f32[8,3072]{1,0:T(8,128)S(1)} %get-tuple-element.213, f32[8,3072]{1,0:T(8,128)S(1)} %multiply_add_fusion.1, f32[8]{0:T(128)S(1)} %div.44), kind=kOutput, calls=%fused_computation.24 | convolution fusion | flops 151068672 | bytes 19169312 | tf_op jit(solution)/shard_map/dot_general | solution.py:131
  795.7 11.0 %gather_fusion.19 = f32[3072,8]{1,0:T(8,128)S(1)} fusion(f32[8,3073]{0,1:T(8,128)} %concatenate.57.clone, s32[3072]{0:T(1024)} %copy-done.45), kind=kCustom, calls=%fused_computation.14.clone | custom fusion | bytes 208896 | tf_op jit(solution)/shard_map/jit(_take)/gather | solution.py:68
  808.8 5.3 collective-permute-start.31
  814.1 4.7 collective-permute-start.33
  818.9 2.9 collective-permute-start.35
  826.8 2.4 bitcast_multiply_fusion
  829.2 13.5 %gather_fusion.20 = f32[3072,8]{1,0:T(8,128)} fusion(f32[8,3072]{0,1:T(8,128)} %bitcast_multiply_fusion, s32[3072]{0:T(1024)} %copy-done.34), kind=kCustom, calls=%fused_computation.9.clone | custom fusion | bytes 208896 | tf_op jit(solution)/shard_map/jit(_take)/gather | solution.py:76
  844.8 38.5 %psum.78 = f32[8]{0:T(128)S(1)} all-reduce(f32[8]{0:T(128)S(1)} %get-tuple-element.158), channel_id=1, replica_groups=mesh['dev'=32] {'dev'}, use_global_device_ids=true, to_apply=%region_24.29 | all-reduce | flops 8 | bytes 64 | tf_op jit(solution)/shard_map/psum | solution.py:148
  884.1 3.2 fusion.22
  887.6 39.3 %psum.79 = f32[192,8]{0,1:T(8,128)S(1)} all-reduce(f32[192,8]{0,1:T(8,128)S(1)} %reshape.531), channel_id=1, replica_groups=mesh['dev'=32] {'dev'}, use_global_device_ids=true, to_apply=%region_25.30 | all-reduce | flops 1536 | bytes 12288 | tf_op jit(solution)/shard_map/psum | solution.py:124
  931.4 10.9 %gather_fusion.21 = f32[3072,8]{1,0:T(8,128)} fusion(f32[8,3072]{0,1:T(8,128)S(1)} %copy.187, s32[3072]{0:T(1024)S(1)} %copy-done.36), kind=kCustom, calls=%fused_computation.10.clone | custom fusion | bytes 208896 | tf_op jit(solution)/shard_map/jit(_take)/gather | solution.py:76
  (455 shorter events, 116.1 us)
Async XLA Ops:
  15.4 289.5 %copy-start.9 = (f32[3072]{0:T(1024)}, f32[3072]{0:T(1024)S(1)}, u32[]{:S(2)}) copy-start(f32[3072]{0:T(1024)S(1)} %get-tuple-element.214) | copy-start | bytes 36868
  26.9 57.4 %copy-start.51 = (f32[1,8,3072]{2,1,0:T(8,128)S(1)}, f32[1,8,3072]{2,1,0:T(8,128)}, u32[]{:S(2)}) copy-start(f32[1,8,3072]{2,1,0:T(8,128)} %param.29) | copy-start | bytes 294916
  28.9 55.9 %copy-start.58 = (pred[6,512]{1,0:T(8,128)(4,1)}, pred[6,512]{1,0:T(8,128)(4,1)S(1)}, u32[]{:S(2)}) copy-start(pred[6,512]{1,0:T(8,128)(4,1)S(1)} %compare_and_fusion.1) | copy-start | bytes 9220
  29.5 67.2 %collective-permute-start = (f32[6,512]{1,0:T(8,128)}, f32[6,512]{1,0:T(8,128)}, u32[]{:S(2)}, u32[]{:S(2)}) collective-permute-start(f32[6,512]{1,0:T(8,128)} %get-tuple-element.199), channel_id=1, source_target_pairs={{0,1},{1,2},{2,3},{3,4},{4,5},{5,6},{6,7},{7,8},{8,9},{9,10},{10,1... | collective-permute-start | bytes 36872 | tf_op jit(solution)/shard_map/ppermute | solution.py:18
  30.0 67.4 %collective-permute-start.1 = (f32[6,512]{1,0:T(8,128)}, f32[6,512]{1,0:T(8,128)}, u32[]{:S(2)}, u32[]{:S(2)}) collective-permute-start(f32[6,512]{1,0:T(8,128)} %get-tuple-element.198), channel_id=1, source_target_pairs={{0,31},{1,0},{2,1},{3,2},{4,3},{5,4},{6,5},{7,6},{8,7},{9,8},{10,9... | collective-permute-start | bytes 36872 | tf_op jit(solution)/shard_map/ppermute | solution.py:18
  36.0 62.2 %collective-permute-start.2 = (f32[6,512]{1,0:T(8,128)}, f32[6,512]{1,0:T(8,128)}, u32[]{:S(2)}, u32[]{:S(2)}) collective-permute-start(f32[6,512]{1,0:T(8,128)} %get-tuple-element.197), channel_id=1, source_target_pairs={{0,4},{1,5},{2,6},{3,7},{4,8},{5,9},{6,10},{7,11},{8,12},{9,13},{1... | collective-permute-start | bytes 36872 | tf_op jit(solution)/shard_map/ppermute | solution.py:18
  36.0 62.9 %collective-permute-start.3 = (f32[6,512]{1,0:T(8,128)}, f32[6,512]{1,0:T(8,128)}, u32[]{:S(2)}, u32[]{:S(2)}) collective-permute-start(f32[6,512]{1,0:T(8,128)} %get-tuple-element.196), channel_id=1, source_target_pairs={{0,28},{1,29},{2,30},{3,31},{4,0},{5,1},{6,2},{7,3},{8,4},{9,5},{1... | collective-permute-start | bytes 36872 | tf_op jit(solution)/shard_map/ppermute | solution.py:18
  40.7 58.9 %collective-permute-start.4 = (f32[6,512]{1,0:T(8,128)}, f32[6,512]{1,0:T(8,128)}, u32[]{:S(2)}, u32[]{:S(2)}) collective-permute-start(f32[6,512]{1,0:T(8,128)} %get-tuple-element.195), channel_id=1, source_target_pairs={{0,16},{1,17},{2,18},{3,19},{4,20},{5,21},{6,22},{7,23},{8,24},{9,... | collective-permute-start | bytes 36872 | tf_op jit(solution)/shard_map/ppermute | solution.py:18
  41.2 310.1 %copy-start.41 = (f32[6,512]{1,0:T(8,128)}, f32[6,512]{1,0:T(8,128)S(1)}, u32[]{:S(2)}) copy-start(f32[6,512]{1,0:T(8,128)S(1)} %fusion.91) | copy-start | bytes 36868
  44.1 183.5 %copy-start.45 = (s32[3072]{0:T(1024)}, s32[3072]{0:T(1024)S(1)}, u32[]{:S(2)}) copy-start(s32[3072]{0:T(1024)S(1)} %get-tuple-element.217) | copy-start | bytes 36868
  44.1 309.5 %copy-start.34 = (s32[3072]{0:T(1024)}, s32[3072]{0:T(1024)S(1)}, u32[]{:S(2)}) copy-start(s32[3072]{0:T(1024)S(1)} %get-tuple-element.216) | copy-start | bytes 36868
  46.3 226.9 %copy-start.54 = (f32[3072]{0:T(1024)}, f32[3072]{0:T(1024)S(1)}, u32[]{:S(2)}) copy-start(f32[3072]{0:T(1024)S(1)} %and_convert_fusion) | copy-start | bytes 36868
  84.3 220.6 %copy-start.17 = (f32[1,3072]{1,0:T(1,128)}, f32[1,3072]{1,0:T(1,128)S(1)}, u32[]{:S(2)}) copy-start(f32[1,3072]{1,0:T(1,128)S(1)} %mul.372) | copy-start | bytes 36868
  96.7 4.6 collective-permute-start.5
  104.8 70.1 %copy-start.56 = (f32[128,64]{1,0:T(8,128)S(1)}, f32[128,64]{1,0:T(8,128)}, u32[]{:S(2)}) copy-start(f32[128,64]{1,0:T(8,128)} %pad_convert_fusion) | copy-start | bytes 98308
  239.2 10.1 %collective-permute-start.6 = (f32[8,512]{1,0:T(8,128)S(1)}, f32[8,512]{1,0:T(8,128)S(1)}, u32[]{:S(2)}, u32[]{:S(2)}) collective-permute-start(f32[8,512]{1,0:T(8,128)S(1)} %get-tuple-element.187), channel_id=1, source_target_pairs={{0,1},{1,2},{2,3},{3,4},{4,5},{5,6},{6,7},{7,8},{8,9},{9,10},{10,1... | collective-permute-start | bytes 49160 | tf_op jit(solution)/shard_map/ppermute | solution.py:18
  239.6 18.3 %collective-permute-start.7 = (f32[8,512]{1,0:T(8,128)S(1)}, f32[8,512]{1,0:T(8,128)S(1)}, u32[]{:S(2)}, u32[]{:S(2)}) collective-permute-start(f32[8,512]{1,0:T(8,128)S(1)} %get-tuple-element.186), channel_id=1, source_target_pairs={{0,31},{1,0},{2,1},{3,2},{4,3},{5,4},{6,5},{7,6},{8,7},{9,8},{10,9... | collective-permute-start | bytes 49160 | tf_op jit(solution)/shard_map/ppermute | solution.py:18
  244.6 13.4 %collective-permute-start.8 = (f32[8,512]{1,0:T(8,128)S(1)}, f32[8,512]{1,0:T(8,128)S(1)}, u32[]{:S(2)}, u32[]{:S(2)}) collective-permute-start(f32[8,512]{1,0:T(8,128)S(1)} %get-tuple-element.185), channel_id=1, source_target_pairs={{0,4},{1,5},{2,6},{3,7},{4,8},{5,9},{6,10},{7,11},{8,12},{9,13},{1... | collective-permute-start | bytes 49160 | tf_op jit(solution)/shard_map/ppermute | solution.py:18
  244.6 13.4 %collective-permute-start.9 = (f32[8,512]{1,0:T(8,128)S(1)}, f32[8,512]{1,0:T(8,128)S(1)}, u32[]{:S(2)}, u32[]{:S(2)}) collective-permute-start(f32[8,512]{1,0:T(8,128)S(1)} %get-tuple-element.184), channel_id=1, source_target_pairs={{0,28},{1,29},{2,30},{3,31},{4,0},{5,1},{6,2},{7,3},{8,4},{9,5},{1... | collective-permute-start | bytes 49160 | tf_op jit(solution)/shard_map/ppermute | solution.py:18
  249.3 13.4 %collective-permute-start.10 = (f32[8,512]{1,0:T(8,128)S(1)}, f32[8,512]{1,0:T(8,128)S(1)}, u32[]{:S(2)}, u32[]{:S(2)}) collective-permute-start(f32[8,512]{1,0:T(8,128)S(1)} %get-tuple-element.183), channel_id=1, source_target_pairs={{0,16},{1,17},{2,18},{3,19},{4,20},{5,21},{6,22},{7,23},{8,24},{9,... | collective-permute-start | bytes 49160 | tf_op jit(solution)/shard_map/ppermute | solution.py:18
  249.3 6.8 collective-permute-start.12
  256.1 6.6 collective-permute-start.11
  257.9 7.8 collective-permute-start.13
  257.9 8.3 collective-permute-start.14
  258.0 8.9 collective-permute-start.15
  262.7 4.8 collective-permute-start.16
  262.7 6.7 collective-permute-start.17
  366.6 63.8 %copy-start.3 = (f32[8,3072]{1,0:T(8,128)}, f32[8,3072]{1,0:T(8,128)S(1)}, u32[]{:S(2)}) copy-start(f32[8,3072]{1,0:T(8,128)S(1)} %fusion.16) | copy-start | bytes 294916
  394.3 10.1 %collective-permute-start.18 = (f32[8,512]{1,0:T(8,128)S(1)}, f32[8,512]{1,0:T(8,128)S(1)}, u32[]{:S(2)}, u32[]{:S(2)}) collective-permute-start(f32[8,512]{1,0:T(8,128)S(1)} %get-tuple-element.181), channel_id=1, source_target_pairs={{0,1},{1,2},{2,3},{3,4},{4,5},{5,6},{6,7},{7,8},{8,9},{9,10},{10,1... | collective-permute-start | bytes 49160 | tf_op jit(solution)/shard_map/ppermute | solution.py:18
  394.4 13.6 %collective-permute-start.19 = (f32[8,512]{1,0:T(8,128)S(1)}, f32[8,512]{1,0:T(8,128)S(1)}, u32[]{:S(2)}, u32[]{:S(2)}) collective-permute-start(f32[8,512]{1,0:T(8,128)S(1)} %get-tuple-element.180), channel_id=1, source_target_pairs={{0,31},{1,0},{2,1},{3,2},{4,3},{5,4},{6,5},{7,6},{8,7},{9,8},{10,9... | collective-permute-start | bytes 49160 | tf_op jit(solution)/shard_map/ppermute | solution.py:18
  399.7 8.9 collective-permute-start.20
  399.7 9.5 %collective-permute-start.21 = (f32[8,512]{1,0:T(8,128)S(1)}, f32[8,512]{1,0:T(8,128)S(1)}, u32[]{:S(2)}, u32[]{:S(2)}) collective-permute-start(f32[8,512]{1,0:T(8,128)S(1)} %get-tuple-element.178), channel_id=1, source_target_pairs={{0,28},{1,29},{2,30},{3,31},{4,0},{5,1},{6,2},{7,3},{8,4},{9,5},{1... | collective-permute-start | bytes 49160 | tf_op jit(solution)/shard_map/ppermute | solution.py:18
  404.4 5.3 collective-permute-start.22
  404.4 5.9 collective-permute-start.23
  414.7 55.0 %copy-start.33 = (f32[8,3072]{1,0:T(8,128)S(1)}, f32[8,3072]{1,0:T(8,128)}, u32[]{:S(2)}) copy-start(f32[8,3072]{1,0:T(8,128)} %copy-done.31) | copy-start | bytes 294916
  469.7 46.6 %copy-start.42 = (f32[6,512]{1,0:T(8,128)S(1)}, f32[6,512]{1,0:T(8,128)}, u32[]{:S(2)}) copy-start(f32[6,512]{1,0:T(8,128)} %copy-done.41) | copy-start | bytes 36868
  469.8 47.5 %copy-start.28 = (f32[8,3072]{1,0:T(8,128)}, f32[8,3072]{1,0:T(8,128)S(1)}, u32[]{:S(2)}) copy-start(f32[8,3072]{1,0:T(8,128)S(1)} %multiply_subtract_fusion.2) | copy-start | bytes 294916
  473.0 45.6 %copy-start.35 = (s32[3072]{0:T(1024)S(1)}, s32[3072]{0:T(1024)}, u32[]{:S(2)}) copy-start(s32[3072]{0:T(1024)} %copy-done.34) | copy-start | bytes 36868
  529.5 43.6 %copy-start.4 = (f32[8,3072]{1,0:T(8,128)S(1)}, f32[8,3072]{1,0:T(8,128)}, u32[]{:S(2)}) copy-start(f32[8,3072]{1,0:T(8,128)} %copy-done.3) | copy-start | bytes 294916
  600.8 10.3 %collective-permute-start.24 = (f32[8,512]{1,0:T(8,128)S(1)}, f32[8,512]{1,0:T(8,128)S(1)}, u32[]{:S(2)}, u32[]{:S(2)}) collective-permute-start(f32[8,512]{1,0:T(8,128)S(1)} %get-tuple-element.175), channel_id=1, source_target_pairs={{0,1},{1,2},{2,3},{3,4},{4,5},{5,6},{6,7},{7,8},{8,9},{9,10},{10,1... | collective-permute-start | bytes 49160 | tf_op jit(solution)/shard_map/ppermute | solution.py:18
  600.9 13.7 %collective-permute-start.25 = (f32[8,512]{1,0:T(8,128)S(1)}, f32[8,512]{1,0:T(8,128)S(1)}, u32[]{:S(2)}, u32[]{:S(2)}) collective-permute-start(f32[8,512]{1,0:T(8,128)S(1)} %get-tuple-element.174), channel_id=1, source_target_pairs={{0,31},{1,0},{2,1},{3,2},{4,3},{5,4},{6,5},{7,6},{8,7},{9,8},{10,9... | collective-permute-start | bytes 49160 | tf_op jit(solution)/shard_map/ppermute | solution.py:18
  606.2 9.0 collective-permute-start.26
  606.2 9.6 %collective-permute-start.27 = (f32[8,512]{1,0:T(8,128)S(1)}, f32[8,512]{1,0:T(8,128)S(1)}, u32[]{:S(2)}, u32[]{:S(2)}) collective-permute-start(f32[8,512]{1,0:T(8,128)S(1)} %get-tuple-element.172), channel_id=1, source_target_pairs={{0,28},{1,29},{2,30},{3,31},{4,0},{5,1},{6,2},{7,3},{8,4},{9,5},{1... | collective-permute-start | bytes 49160 | tf_op jit(solution)/shard_map/ppermute | solution.py:18
  611.1 5.3 collective-permute-start.28
  611.1 5.9 collective-permute-start.29
  621.4 54.0 %copy-start.78 = (f32[8]{0:T(128)S(1)}, f32[8]{0:T(128)}, u32[]{:S(2)}) copy-start(f32[8]{0:T(128)} %copy-done.77) | copy-start | bytes 100
  621.4 54.0 %copy-start.30 = (f32[8,3072]{1,0:T(8,128)S(1)}, f32[8,3072]{1,0:T(8,128)}, u32[]{:S(2)}) copy-start(f32[8,3072]{1,0:T(8,128)} %copy-done.28) | copy-start | bytes 294916
  675.4 43.6 %copy-start.72 = (f32[8]{0:T(128)}, f32[8]{0:T(128)S(1)}, u32[]{:S(2)}) copy-start(f32[8]{0:T(128)S(1)} %div.43) | copy-start | bytes 100
  675.4 47.8 %copy-start.43 = (f32[6,512]{1,0:T(8,128)S(1)}, f32[6,512]{1,0:T(8,128)}, u32[]{:S(2)}) copy-start(f32[6,512]{1,0:T(8,128)} %copy-done.41) | copy-start | bytes 36868
  737.5 43.1 %copy-start.79 = (f32[8]{0:T(128)S(1)}, f32[8]{0:T(128)}, u32[]{:S(2)}) copy-start(f32[8]{0:T(128)} %copy-done.77) | copy-start | bytes 100
  808.7 10.1 %collective-permute-start.30 = (f32[8,512]{1,0:T(8,128)S(1)}, f32[8,512]{1,0:T(8,128)S(1)}, u32[]{:S(2)}, u32[]{:S(2)}) collective-permute-start(f32[8,512]{1,0:T(8,128)S(1)} %get-tuple-element.169), channel_id=1, source_target_pairs={{0,1},{1,2},{2,3},{3,4},{4,5},{5,6},{6,7},{7,8},{8,9},{9,10},{10,1... | collective-permute-start | bytes 49160 | tf_op jit(solution)/shard_map/ppermute | solution.py:18
  808.8 13.6 %collective-permute-start.31 = (f32[8,512]{1,0:T(8,128)S(1)}, f32[8,512]{1,0:T(8,128)S(1)}, u32[]{:S(2)}, u32[]{:S(2)}) collective-permute-start(f32[8,512]{1,0:T(8,128)S(1)} %get-tuple-element.168), channel_id=1, source_target_pairs={{0,31},{1,0},{2,1},{3,2},{4,3},{5,4},{6,5},{7,6},{8,7},{9,8},{10,9... | collective-permute-start | bytes 49160 | tf_op jit(solution)/shard_map/ppermute | solution.py:18
  814.1 8.9 collective-permute-start.32
  814.1 9.5 %collective-permute-start.33 = (f32[8,512]{1,0:T(8,128)S(1)}, f32[8,512]{1,0:T(8,128)S(1)}, u32[]{:S(2)}, u32[]{:S(2)}) collective-permute-start(f32[8,512]{1,0:T(8,128)S(1)} %get-tuple-element.166), channel_id=1, source_target_pairs={{0,28},{1,29},{2,30},{3,31},{4,0},{5,1},{6,2},{7,3},{8,4},{9,5},{1... | collective-permute-start | bytes 49160 | tf_op jit(solution)/shard_map/ppermute | solution.py:18
  818.9 5.3 collective-permute-start.34
  818.9 5.9 collective-permute-start.35
  829.2 54.2 %copy-start.81 = (f32[8]{0:T(128)S(1)}, f32[8]{0:T(128)}, u32[]{:S(2)}) copy-start(f32[8]{0:T(128)} %copy-done.80) | copy-start | bytes 100
  829.2 54.2 %copy-start.5 = (f32[8,3072]{1,0:T(8,128)S(1)}, f32[8,3072]{1,0:T(8,128)}, u32[]{:S(2)}) copy-start(f32[8,3072]{1,0:T(8,128)} %copy-done.3) | copy-start | bytes 294916
  829.2 54.2 %copy-start.40 = (f32[8,3072]{1,0:T(8,128)S(1)}, f32[8,3072]{1,0:T(8,128)}, u32[]{:S(2)}) copy-start(f32[8,3072]{1,0:T(8,128)} %copy-done.39) | copy-start | bytes 294916
  829.2 54.2 %copy-start.71 = (f32[8]{0:T(128)S(1)}, f32[8]{0:T(128)}, u32[]{:S(2)}) copy-start(f32[8]{0:T(128)} %copy-done.70) | copy-start | bytes 100
  829.2 54.2 %copy-start.73 = (f32[8]{0:T(128)S(1)}, f32[8]{0:T(128)}, u32[]{:S(2)}) copy-start(f32[8]{0:T(128)} %copy-done.72) | copy-start | bytes 100
  842.7 41.5 %copy-start.8 = (f32[8,3072]{1,0:T(8,128)S(1)}, f32[8,3072]{1,0:T(8,128)}, u32[]{:S(2)}) copy-start(f32[8,3072]{1,0:T(8,128)} %copy-done.6) | copy-start | bytes 294916
  883.4 47.3 %copy-start.44 = (f32[6,512]{1,0:T(8,128)S(1)}, f32[6,512]{1,0:T(8,128)}, u32[]{:S(2)}) copy-start(f32[6,512]{1,0:T(8,128)} %copy-done.41) | copy-start | bytes 36868
  887.4 44.1 %copy-start.36 = (s32[3072]{0:T(1024)S(1)}, s32[3072]{0:T(1024)}, u32[]{:S(2)}) copy-start(s32[3072]{0:T(1024)} %copy-done.34) | copy-start | bytes 36868
  (54 other events, 582.0 us)
where the time goes:
time: 954 us; the launch traced here: 945 us
  blocking collectives  429 us (45%)
  local copies, waits for them, and re-layouts  283 us (30%)
  matrix products  80.1 us (8%)
  other arithmetic  72 us (8%)
  starting transfers between devices  69.4 us (7%)
    psum x4, blocking collectives, project(): coarse_all = lax.psum(placed, 'dev').reshape(devices * MODES, loads)  156 us
    gather x20, local copies, waits for them, and re-layouts, spread_back(): return jnp.take(flattened, dof_codes, axis=1) * shared_float[None]  139 us
    psum x3, blocking collectives, project(): norm_sq = lax.psum(partial_inner(projected, projected), 'dev')  120 us
    psum x2, blocking collectives, per_device(): curvature = lax.psum(partial_inner(direction, applied), 'dev')  77 us
    gather x12, local copies, waits for them, and re-layouts, gather_faces(): return jnp.take(padded, inverse, axis=1)  70.2 us
    ppermute x36, starting transfers between devices, from_behind(): lax.ppermute(value, axis, [(i, (i + by) % length) for i in range(length)])  69.4 us
    dot_general x4, matrix products, dual_apply(): lax.dot_general(vector.astype(jnp.bfloat16), dual_blocks[0], (((1,), (1,)...  47.9 us
    all_gather x1, blocking collectives, per_device(): lax.all_gather(block_row.reshape(MODES, devices * MODES), 'dev', axis=0,...  39.5 us
  transfers between devices with their start and end apart: 36, of which 2 were waited for; matrix products, arithmetic and copies ran while one was open for 4% of the time, Pallas kernels for 0%

commit v1 on v0

--- a/solution.py
+++ b/solution.py
@@ -124,7 +124,7 @@
         coarse_all = lax.psum(placed, "dev").reshape(devices * MODES, loads)
         solution = solve_coarse(factor, coarse_all)
         projected = residual - modes_apply(solution)
-        norm_sq = lax.psum(partial_inner(projected, projected), "dev")
+        norm_sq = jnp.sum(lax.all_gather(partial_inner(projected, projected), "dev"), axis=0)
         return (projected, norm_sq)
 
     def dual_apply(vector):

time: 954 us -> 955 us (level)
    psum x3 -> x0, blocking collectives: 120 us -> none  [project(): norm_sq = lax.psum(partial_inner(projected, projected), 'dev')]
    unnamed x0 -> x3, blocking collectives: none -> 120 us
    unnamed x203 -> x209, local copies, waits for them, and re-layouts: 27.1 us -> 27.7 us
where the time goes in v1:
time: 955 us; the launch traced here: 946 us
  blocking collectives  429 us (45%)
  local copies, waits for them, and re-layouts  283 us (30%)
  matrix products  80.5 us (8%)
  other arithmetic  72.2 us (8%)
  starting transfers between devices  69.4 us (7%)
    psum x4, blocking collectives, project(): coarse_all = lax.psum(placed, 'dev').reshape(devices * MODES, loads)  156 us
    gather x20, local copies, waits for them, and re-layouts, spread_back(): return jnp.take(flattened, dof_codes, axis=1) * shared_float[None]  138 us
    unnamed x3, blocking collectives  120 us
    psum x2, blocking collectives, per_device(): curvature = lax.psum(partial_inner(direction, applied), 'dev')  77 us
    gather x12, local copies, waits for them, and re-layouts, gather_faces(): return jnp.take(padded, inverse, axis=1)  70.2 us
    ppermute x36, starting transfers between devices, from_behind(): lax.ppermute(value, axis, [(i, (i + by) % length) for i in range(length)])  69.4 us
    dot_general x4, matrix products, dual_apply(): lax.dot_general(vector.astype(jnp.bfloat16), dual_blocks[0], (((1,), (1,)...  48 us
    all_gather x1, blocking collectives, per_device(): lax.all_gather(block_row.reshape(MODES, devices * MODES), 'dev', axis=0,...  39.5 us
  transfers between devices with their start and end apart: 36, of which 2 were waited for; matrix products, arithmetic and copies ran while one was open for 4% of the time, Pallas kernels for 0%

profile of v1, /device:TPU:0, one launch (start us, length us, event | category | flops | bytes accessed | tf_op | source)
XLA Modules:
  0.0 946.2 jit_solution(17464302292947022002)
XLA Ops:
  2.1 11.8 %scatter_custom_fusion = s32[3072]{0:T(1024)S(1)} fusion(s32[3072]{0:T(1024)S(1)} %bitcast.527, s32[3072]{0:T(1024)S(1)} %iota.115, s32[]{:T(128)} %constant.261.clone.1), kind=kCustom, calls=%fused_computation.314 | custom fusion | bytes 12292 | tf_op jit(solution)/shard_map/scatter | solution.py:58
  16.0 10.8 %gather_fusion.1 = f32[3072,6]{1,0:T(8,128)} fusion(f32[6,3073]{0,1:T(8,128)S(1)} %concatenate.51, s32[3072]{0:T(1024)S(1)} %broadcast_clamp_fusion.1), kind=kCustom, calls=%fused_computation.16 | custom fusion | bytes 159744 | tf_op jit(solution)/shard_map/jit(_take)/gather | solution.py:68
  26.8 1.9 copy.135
  30.0 5.9 collective-permute-start.1
  35.9 4.7 collective-permute-start.3
  47.8 36.6 %all-gather = f32[1,192,8]{2,0,1:T(1,128)S(1)} all-gather(f32[1,6,8]{2,0,1:T(1,128)S(1)} %copy-done.67), channel_id=2, replica_groups=mesh['dev'=32] {'dev'}, dimensions={1}, use_global_device_ids=true | all-gather | bytes 6336 | tf_op jit(solution)/shard_map/all_gather | solution.py:105
  86.2 9.5 %gather_fusion.8 = f32[3072,8]{1,0:T(8,128)S(1)} fusion(f32[8,3073]{0,1:T(8,128)} %concatenate.52.clone, s32[3072]{0:T(1024)S(1)} %get-tuple-element.217), kind=kCustom, calls=%fused_computation.1.clone | custom fusion | bytes 208896 | tf_op jit(solution)/shard_map/jit(_take)/gather | solution.py:68
  101.9 2.0 scatter_fusion
  104.9 39.5 %all-gather.4 = f32[32,6,192]{2,1,0:T(8,128)S(1)} all-gather(f32[1,6,192]{2,1,0:T(8,128)S(1)} %reshape.904), channel_id=1, replica_groups=mesh['dev'=32] {'dev'}, dimensions={0}, use_global_device_ids=true | all-gather | bytes 152064 | tf_op jit(solution)/shard_map/all_gather | solution.py:104
  144.6 11.7 %cholesky.51 = f32[128,128]{1,0:T(8,128)S(1)} custom-call(f32[128,128]{1,0:T(8,128)S(1)} %cholesky.124), custom_call_target="Cholesky" | custom-call | tf_op jit(solution)/shard_map/jit(cholesky)/cholesky | solution.py:107
  156.4 9.8 %custom-call.17 = f32[1,128,128]{1,2,0:T(8,128)S(1)} custom-call(f32[1,128,128]{2,1,0:T(8,128)S(1)} %get-tuple-element.201), custom_call_target="InvertDiagBlocksLowerTriangular" | custom-call | tf_op jit(solution)/shard_map/jit(cholesky)/cholesky | solution.py:107
  166.6 5.8 cholesky.110
  175.3 19.8 %custom-call.27 = f32[2,128,128]{1,2,0:T(8,128)S(1)} custom-call(f32[2,128,128]{2,1,0:T(8,128)S(1)} %pad_maximum_fusion), custom_call_target="InvertDiagBlocksLowerTriangular" | custom-call | tf_op jit(solution)/shard_map/triangular_solve/custom-call.4 | solution.py:23
  199.6 10.8 %gather_fusion.7 = f32[3072,8]{1,0:T(8,128)} fusion(f32[8,3072]{0,1:T(8,128)S(1)} %copy.143, s32[3072]{0:T(1024)S(1)} %get-tuple-element.216), kind=kCustom, calls=%fused_computation.clone | custom fusion | bytes 208896 | tf_op jit(solution)/shard_map/jit(_take)/gather | solution.py:76
  213.2 12.0 %fusion.6 = f32[8,3072]{1,0:T(8,128)} fusion(bf16[1,3072,3072]{2,1,0:T(8,128)(2,1)} %param.27, f32[8,3072]{1,0:T(8,128)S(1)} %fusion.17), kind=kOutput, calls=%fused_computation.30 | convolution fusion | flops 151019520 | bytes 19070976 | tf_op jit(solution)/shard_map/dot_general | solution.py:131
  227.8 9.5 %gather_fusion.10 = f32[3072,8]{1,0:T(8,128)S(1)} fusion(f32[8,3073]{0,1:T(8,128)} %concatenate.53.clone, s32[3072]{0:T(1024)S(1)} %get-tuple-element.217), kind=kCustom, calls=%fused_computation.11.clone | custom fusion | bytes 208896 | tf_op jit(solution)/shard_map/jit(_take)/gather | solution.py:68
  239.8 5.0 collective-permute-start.7
  244.8 4.7 collective-permute-start.9
  249.6 6.7 collective-permute-done.12
  258.2 4.7 collective-permute-start.15
  262.9 2.9 collective-permute-start.17
  271.0 2.5 copy.151
  273.5 3.7 bitcast_multiply_fusion.4
  277.2 12.6 %gather_fusion.11 = f32[3072,8]{1,0:T(8,128)} fusion(f32[8,3072]{0,1:T(8,128)} %get-tuple-element.205, s32[3072]{0:T(1024)S(1)} %get-tuple-element.216), kind=kCustom, calls=%fused_computation.3.clone | custom fusion | bytes 208896 | tf_op jit(solution)/shard_map/jit(_take)/gather | solution.py:76
  289.8 2.5 copy.152
  292.3 10.8 %gather_fusion.9 = f32[3072,8]{1,0:T(8,128)} fusion(f32[8,3072]{0,1:T(8,128)S(1)} %copy-done.2, s32[3072]{0:T(1024)S(1)} %get-tuple-element.216), kind=kCustom, calls=%fused_computation.2.clone | custom fusion | bytes 208896 | tf_op jit(solution)/shard_map/jit(_take)/gather | solution.py:76
  305.7 3.3 fusion.19
  309.3 37.9 %psum.49 = f32[192,8]{0,1:T(8,128)S(1)} all-reduce(f32[192,8]{0,1:T(8,128)S(1)} %reshape.527), channel_id=1, replica_groups=mesh['dev'=32] {'dev'}, use_global_device_ids=true, to_apply=%region_10.15 | all-reduce | flops 1536 | bytes 12288 | tf_op jit(solution)/shard_map/psum | solution.py:124
  353.7 10.8 %gather_fusion.12 = f32[3072,8]{1,0:T(8,128)} fusion(f32[8,3072]{0,1:T(8,128)S(1)} %copy.157, s32[3072]{0:T(1024)S(1)} %get-tuple-element.216), kind=kCustom, calls=%fused_computation.4.clone | custom fusion | bytes 208896 | tf_op jit(solution)/shard_map/jit(_take)/gather | solution.py:76
  366.7 12.0 %fusion.4 = f32[8,3072]{1,0:T(8,128)} fusion(bf16[1,3072,3072]{2,1,0:T(8,128)(2,1)} %param.27, f32[8,3072]{1,0:T(8,128)S(1)} %fusion.16), kind=kOutput, calls=%fused_computation.28 | convolution fusion | flops 151019520 | bytes 19070976 | tf_op jit(solution)/shard_map/dot_general | solution.py:131
  381.4 11.0 %gather_fusion.13 = f32[3072,8]{1,0:T(8,128)S(1)} fusion(f32[8,3073]{0,1:T(8,128)} %concatenate.55.clone, s32[3072]{0:T(1024)} %copy-done.45), kind=kCustom, calls=%fused_computation.12.clone | custom fusion | bytes 208896 | tf_op jit(solution)/shard_map/jit(_take)/gather | solution.py:68
  394.5 5.3 collective-permute-start.19
  399.8 4.7 collective-permute-start.21
  404.5 2.9 collective-permute-start.23
  412.4 2.4 bitcast_multiply_fusion.2
  414.8 13.7 %gather_fusion.14 = f32[3072,8]{1,0:T(8,128)} fusion(f32[8,3072]{0,1:T(8,128)} %bitcast_multiply_fusion.2, s32[3072]{0:T(1024)} %copy-done.34), kind=kCustom, calls=%fused_computation.5.clone | custom fusion | bytes 208896 | tf_op jit(solution)/shard_map/jit(_take)/gather | solution.py:76
  430.8 38.4 %all-reduce.14 = (f32[256]{0:T(256)S(1)}, f32[8]{0:T(128)S(1)}) all-reduce(f32[256]{0:T(256)S(1)} %dynamic-update-slice.26, f32[8]{0:T(128)S(1)} %get-tuple-element.154), channel_id=3, replica_groups=mesh['dev'=32] {'dev'}, use_global_device_ids=true, to_apply=%add.11 | all-reduce | flops 264 | bytes 2112
  470.0 3.3 fusion.20
  473.6 39.3 %psum.51 = f32[192,8]{0,1:T(8,128)S(1)} all-reduce(f32[192,8]{0,1:T(8,128)S(1)} %reshape.531), channel_id=1, replica_groups=mesh['dev'=32] {'dev'}, use_global_device_ids=true, to_apply=%region_15.20 | all-reduce | flops 1536 | bytes 12288 | tf_op jit(solution)/shard_map/psum | solution.py:124
  519.0 10.8 %gather_fusion.15 = f32[3072,8]{1,0:T(8,128)} fusion(f32[8,3072]{0,1:T(8,128)S(1)} %copy.167, s32[3072]{0:T(1024)S(1)} %copy-done.35), kind=kCustom, calls=%fused_computation.6.clone | custom fusion | bytes 208896 | tf_op jit(solution)/shard_map/jit(_take)/gather | solution.py:76
  532.3 40.7 %all-reduce.12 = f32[256]{0:T(256)S(1)} all-reduce(f32[256]{0:T(256)S(1)} %dynamic-update-slice.27), channel_id=4, replica_groups=mesh['dev'=32] {'dev'}, use_global_device_ids=true, to_apply=%add.12 | all-reduce | flops 256 | bytes 2048
  573.7 12.0 %fusion.2 = f32[8,3072]{1,0:T(8,128)} fusion(bf16[1,3072,3072]{2,1,0:T(8,128)(2,1)} %param.27, f32[8,3072]{1,0:T(8,128)S(1)} %multiply_add_fusion.1), kind=kOutput, calls=%fused_computation.26 | convolution fusion | flops 151019520 | bytes 19070976 | tf_op jit(solution)/shard_map/dot_general | solution.py:131
  588.3 11.0 %gather_fusion.16 = f32[3072,8]{1,0:T(8,128)S(1)} fusion(f32[8,3073]{0,1:T(8,128)} %concatenate.56.clone, s32[3072]{0:T(1024)} %copy-done.45), kind=kCustom, calls=%fused_computation.13.clone | custom fusion | bytes 208896 | tf_op jit(solution)/shard_map/jit(_take)/gather | solution.py:68
  601.6 5.3 collective-permute-start.25
  606.9 4.7 collective-permute-start.27
  611.6 2.9 collective-permute-start.29
  619.5 2.4 bitcast_multiply_fusion.1
  621.9 13.4 %gather_fusion.17 = f32[3072,8]{1,0:T(8,128)} fusion(f32[8,3072]{0,1:T(8,128)} %bitcast_multiply_fusion.1, s32[3072]{0:T(1024)} %copy-done.34), kind=kCustom, calls=%fused_computation.7.clone | custom fusion | bytes 208896 | tf_op jit(solution)/shard_map/jit(_take)/gather | solution.py:76
  637.3 38.5 %psum.52 = f32[8]{0:T(128)S(1)} all-reduce(f32[8]{0:T(128)S(1)} %multiply_reduce_fusion.1), channel_id=1, replica_groups=mesh['dev'=32] {'dev'}, use_global_device_ids=true, to_apply=%region_19.24 | all-reduce | flops 8 | bytes 64 | tf_op jit(solution)/shard_map/psum | solution.py:148
  676.5 3.3 fusion.21
  680.1 39.3 %psum.53 = f32[192,8]{0,1:T(8,128)S(1)} all-reduce(f32[192,8]{0,1:T(8,128)S(1)} %reshape.535), channel_id=1, replica_groups=mesh['dev'=32] {'dev'}, use_global_device_ids=true, to_apply=%region_20.25 | all-reduce | flops 1536 | bytes 12288 | tf_op jit(solution)/shard_map/psum | solution.py:124
  726.0 11.8 %gather_fusion.18 = f32[3072,8]{1,0:T(8,128)} fusion(f32[8,3072]{0,1:T(8,128)S(1)} %copy.177, s32[3072]{0:T(1024)} %copy-done.34), kind=kCustom, calls=%fused_computation.8.clone | custom fusion | bytes 208896 | tf_op jit(solution)/shard_map/jit(_take)/gather | solution.py:76
  740.5 40.9 %all-reduce.13 = f32[256]{0:T(256)S(1)} all-reduce(f32[256]{0:T(256)S(1)} %dynamic-update-slice.28), channel_id=5, replica_groups=mesh['dev'=32] {'dev'}, use_global_device_ids=true, to_apply=%add.13 | all-reduce | flops 256 | bytes 2048
  782.1 12.0 %fusion = f32[8,3072]{1,0:T(8,128)} fusion(bf16[1,3072,3072]{2,1,0:T(8,128)(2,1)} %param.27, f32[8,3072]{1,0:T(8,128)S(1)} %get-tuple-element.213, f32[8,3072]{1,0:T(8,128)S(1)} %multiply_add_fusion.1, f32[8]{0:T(128)S(1)} %div.52), kind=kOutput, calls=%fused_computation.24 | convolution fusion | flops 151068672 | bytes 19169312 | tf_op jit(solution)/shard_map/dot_general | solution.py:131
  796.7 11.0 %gather_fusion.19 = f32[3072,8]{1,0:T(8,128)S(1)} fusion(f32[8,3073]{0,1:T(8,128)} %concatenate.57.clone, s32[3072]{0:T(1024)} %copy-done.45), kind=kCustom, calls=%fused_computation.14.clone | custom fusion | bytes 208896 | tf_op jit(solution)/shard_map/jit(_take)/gather | solution.py:68
  809.8 5.3 collective-permute-start.31
  815.1 4.7 collective-permute-start.33
  819.8 2.9 collective-permute-start.35
  827.7 2.4 bitcast_multiply_fusion
  830.2 13.4 %gather_fusion.20 = f32[3072,8]{1,0:T(8,128)} fusion(f32[8,3072]{0,1:T(8,128)} %bitcast_multiply_fusion, s32[3072]{0:T(1024)} %copy-done.34), kind=kCustom, calls=%fused_computation.9.clone | custom fusion | bytes 208896 | tf_op jit(solution)/shard_map/jit(_take)/gather | solution.py:76
  845.7 38.5 %psum.54 = f32[8]{0:T(128)S(1)} all-reduce(f32[8]{0:T(128)S(1)} %get-tuple-element.158), channel_id=1, replica_groups=mesh['dev'=32] {'dev'}, use_global_device_ids=true, to_apply=%region_24.29 | all-reduce | flops 8 | bytes 64 | tf_op jit(solution)/shard_map/psum | solution.py:148
  885.1 3.3 fusion.22
  888.6 39.3 %psum.55 = f32[192,8]{0,1:T(8,128)S(1)} all-reduce(f32[192,8]{0,1:T(8,128)S(1)} %reshape.539), channel_id=1, replica_groups=mesh['dev'=32] {'dev'}, use_global_device_ids=true, to_apply=%region_25.30 | all-reduce | flops 1536 | bytes 12288 | tf_op jit(solution)/shard_map/psum | solution.py:124
  932.4 10.8 %gather_fusion.21 = f32[3072,8]{1,0:T(8,128)} fusion(f32[8,3072]{0,1:T(8,128)S(1)} %copy.187, s32[3072]{0:T(1024)S(1)} %copy-done.36), kind=kCustom, calls=%fused_computation.10.clone | custom fusion | bytes 208896 | tf_op jit(solution)/shard_map/jit(_take)/gather | solution.py:76
  (467 shorter events, 117.4 us)
Async XLA Ops:
  15.4 289.6 %copy-start.9 = (f32[3072]{0:T(1024)}, f32[3072]{0:T(1024)S(1)}, u32[]{:S(2)}) copy-start(f32[3072]{0:T(1024)S(1)} %get-tuple-element.214) | copy-start | bytes 36868
  26.8 57.6 %copy-start.51 = (f32[1,8,3072]{2,1,0:T(8,128)S(1)}, f32[1,8,3072]{2,1,0:T(8,128)}, u32[]{:S(2)}) copy-start(f32[1,8,3072]{2,1,0:T(8,128)} %param.29) | copy-start | bytes 294916
  28.8 56.1 %copy-start.58 = (pred[6,512]{1,0:T(8,128)(4,1)}, pred[6,512]{1,0:T(8,128)(4,1)S(1)}, u32[]{:S(2)}) copy-start(pred[6,512]{1,0:T(8,128)(4,1)S(1)} %compare_and_fusion.1) | copy-start | bytes 9220
  29.5 67.4 %collective-permute-start = (f32[6,512]{1,0:T(8,128)}, f32[6,512]{1,0:T(8,128)}, u32[]{:S(2)}, u32[]{:S(2)}) collective-permute-start(f32[6,512]{1,0:T(8,128)} %get-tuple-element.199), channel_id=1, source_target_pairs={{0,1},{1,2},{2,3},{3,4},{4,5},{5,6},{6,7},{7,8},{8,9},{9,10},{10,1... | collective-permute-start | bytes 36872 | tf_op jit(solution)/shard_map/ppermute | solution.py:18
  30.0 67.6 %collective-permute-start.1 = (f32[6,512]{1,0:T(8,128)}, f32[6,512]{1,0:T(8,128)}, u32[]{:S(2)}, u32[]{:S(2)}) collective-permute-start(f32[6,512]{1,0:T(8,128)} %get-tuple-element.198), channel_id=1, source_target_pairs={{0,31},{1,0},{2,1},{3,2},{4,3},{5,4},{6,5},{7,6},{8,7},{9,8},{10,9... | collective-permute-start | bytes 36872 | tf_op jit(solution)/shard_map/ppermute | solution.py:18
  35.9 62.4 %collective-permute-start.2 = (f32[6,512]{1,0:T(8,128)}, f32[6,512]{1,0:T(8,128)}, u32[]{:S(2)}, u32[]{:S(2)}) collective-permute-start(f32[6,512]{1,0:T(8,128)} %get-tuple-element.197), channel_id=1, source_target_pairs={{0,4},{1,5},{2,6},{3,7},{4,8},{5,9},{6,10},{7,11},{8,12},{9,13},{1... | collective-permute-start | bytes 36872 | tf_op jit(solution)/shard_map/ppermute | solution.py:18
  35.9 63.1 %collective-permute-start.3 = (f32[6,512]{1,0:T(8,128)}, f32[6,512]{1,0:T(8,128)}, u32[]{:S(2)}, u32[]{:S(2)}) collective-permute-start(f32[6,512]{1,0:T(8,128)} %get-tuple-element.196), channel_id=1, source_target_pairs={{0,28},{1,29},{2,30},{3,31},{4,0},{5,1},{6,2},{7,3},{8,4},{9,5},{1... | collective-permute-start | bytes 36872 | tf_op jit(solution)/shard_map/ppermute | solution.py:18
  40.6 59.1 %collective-permute-start.4 = (f32[6,512]{1,0:T(8,128)}, f32[6,512]{1,0:T(8,128)}, u32[]{:S(2)}, u32[]{:S(2)}) collective-permute-start(f32[6,512]{1,0:T(8,128)} %get-tuple-element.195), channel_id=1, source_target_pairs={{0,16},{1,17},{2,18},{3,19},{4,20},{5,21},{6,22},{7,23},{8,24},{9,... | collective-permute-start | bytes 36872 | tf_op jit(solution)/shard_map/ppermute | solution.py:18
  41.1 310.3 %copy-start.41 = (f32[6,512]{1,0:T(8,128)}, f32[6,512]{1,0:T(8,128)S(1)}, u32[]{:S(2)}) copy-start(f32[6,512]{1,0:T(8,128)S(1)} %fusion.91) | copy-start | bytes 36868
  44.2 183.6 %copy-start.45 = (s32[3072]{0:T(1024)}, s32[3072]{0:T(1024)S(1)}, u32[]{:S(2)}) copy-start(s32[3072]{0:T(1024)S(1)} %get-tuple-element.217) | copy-start | bytes 36868
  44.2 309.6 %copy-start.34 = (s32[3072]{0:T(1024)}, s32[3072]{0:T(1024)S(1)}, u32[]{:S(2)}) copy-start(s32[3072]{0:T(1024)S(1)} %get-tuple-element.216) | copy-start | bytes 36868
  46.5 227.0 %copy-start.54 = (f32[3072]{0:T(1024)}, f32[3072]{0:T(1024)S(1)}, u32[]{:S(2)}) copy-start(f32[3072]{0:T(1024)S(1)} %and_convert_fusion) | copy-start | bytes 36868
  84.4 220.5 %copy-start.17 = (f32[1,3072]{1,0:T(1,128)}, f32[1,3072]{1,0:T(1,128)S(1)}, u32[]{:S(2)}) copy-start(f32[1,3072]{1,0:T(1,128)S(1)} %mul.372) | copy-start | bytes 36868
  96.8 4.6 collective-permute-start.5
  104.9 70.2 %copy-start.56 = (f32[128,64]{1,0:T(8,128)S(1)}, f32[128,64]{1,0:T(8,128)}, u32[]{:S(2)}) copy-start(f32[128,64]{1,0:T(8,128)} %pad_convert_fusion) | copy-start | bytes 98308
  239.4 10.1 %collective-permute-start.6 = (f32[8,512]{1,0:T(8,128)S(1)}, f32[8,512]{1,0:T(8,128)S(1)}, u32[]{:S(2)}, u32[]{:S(2)}) collective-permute-start(f32[8,512]{1,0:T(8,128)S(1)} %get-tuple-element.187), channel_id=1, source_target_pairs={{0,1},{1,2},{2,3},{3,4},{4,5},{5,6},{6,7},{7,8},{8,9},{9,10},{10,1... | collective-permute-start | bytes 49160 | tf_op jit(solution)/shard_map/ppermute | solution.py:18
  239.8 18.3 %collective-permute-start.7 = (f32[8,512]{1,0:T(8,128)S(1)}, f32[8,512]{1,0:T(8,128)S(1)}, u32[]{:S(2)}, u32[]{:S(2)}) collective-permute-start(f32[8,512]{1,0:T(8,128)S(1)} %get-tuple-element.186), channel_id=1, source_target_pairs={{0,31},{1,0},{2,1},{3,2},{4,3},{5,4},{6,5},{7,6},{8,7},{9,8},{10,9... | collective-permute-start | bytes 49160 | tf_op jit(solution)/shard_map/ppermute | solution.py:18
  244.8 13.4 %collective-permute-start.8 = (f32[8,512]{1,0:T(8,128)S(1)}, f32[8,512]{1,0:T(8,128)S(1)}, u32[]{:S(2)}, u32[]{:S(2)}) collective-permute-start(f32[8,512]{1,0:T(8,128)S(1)} %get-tuple-element.185), channel_id=1, source_target_pairs={{0,4},{1,5},{2,6},{3,7},{4,8},{5,9},{6,10},{7,11},{8,12},{9,13},{1... | collective-permute-start | bytes 49160 | tf_op jit(solution)/shard_map/ppermute | solution.py:18
  244.8 13.4 %collective-permute-start.9 = (f32[8,512]{1,0:T(8,128)S(1)}, f32[8,512]{1,0:T(8,128)S(1)}, u32[]{:S(2)}, u32[]{:S(2)}) collective-permute-start(f32[8,512]{1,0:T(8,128)S(1)} %get-tuple-element.184), channel_id=1, source_target_pairs={{0,28},{1,29},{2,30},{3,31},{4,0},{5,1},{6,2},{7,3},{8,4},{9,5},{1... | collective-permute-start | bytes 49160 | tf_op jit(solution)/shard_map/ppermute | solution.py:18
  249.5 13.4 %collective-permute-start.10 = (f32[8,512]{1,0:T(8,128)S(1)}, f32[8,512]{1,0:T(8,128)S(1)}, u32[]{:S(2)}, u32[]{:S(2)}) collective-permute-start(f32[8,512]{1,0:T(8,128)S(1)} %get-tuple-element.183), channel_id=1, source_target_pairs={{0,16},{1,17},{2,18},{3,19},{4,20},{5,21},{6,22},{7,23},{8,24},{9,... | collective-permute-start | bytes 49160 | tf_op jit(solution)/shard_map/ppermute | solution.py:18
  249.5 6.8 collective-permute-start.12
  256.3 6.6 collective-permute-start.11
  258.1 7.8 collective-permute-start.13
  258.1 8.3 collective-permute-start.14
  258.2 8.9 collective-permute-start.15
  262.9 4.8 collective-permute-start.16
  262.9 6.7 collective-permute-start.17
  366.7 63.7 %copy-start.3 = (f32[8,3072]{1,0:T(8,128)}, f32[8,3072]{1,0:T(8,128)S(1)}, u32[]{:S(2)}) copy-start(f32[8,3072]{1,0:T(8,128)S(1)} %fusion.16) | copy-start | bytes 294916
  394.4 10.1 %collective-permute-start.18 = (f32[8,512]{1,0:T(8,128)S(1)}, f32[8,512]{1,0:T(8,128)S(1)}, u32[]{:S(2)}, u32[]{:S(2)}) collective-permute-start(f32[8,512]{1,0:T(8,128)S(1)} %get-tuple-element.181), channel_id=1, source_target_pairs={{0,1},{1,2},{2,3},{3,4},{4,5},{5,6},{6,7},{7,8},{8,9},{9,10},{10,1... | collective-permute-start | bytes 49160 | tf_op jit(solution)/shard_map/ppermute | solution.py:18
  394.5 13.6 %collective-permute-start.19 = (f32[8,512]{1,0:T(8,128)S(1)}, f32[8,512]{1,0:T(8,128)S(1)}, u32[]{:S(2)}, u32[]{:S(2)}) collective-permute-start(f32[8,512]{1,0:T(8,128)S(1)} %get-tuple-element.180), channel_id=1, source_target_pairs={{0,31},{1,0},{2,1},{3,2},{4,3},{5,4},{6,5},{7,6},{8,7},{9,8},{10,9... | collective-permute-start | bytes 49160 | tf_op jit(solution)/shard_map/ppermute | solution.py:18
  399.8 8.9 collective-permute-start.20
  399.8 9.5 collective-permute-start.21
  404.5 5.3 collective-permute-start.22
  404.5 6.0 collective-permute-start.23
  414.8 55.1 %copy-start.33 = (f32[8,3072]{1,0:T(8,128)S(1)}, f32[8,3072]{1,0:T(8,128)}, u32[]{:S(2)}) copy-start(f32[8,3072]{1,0:T(8,128)} %copy-done.31) | copy-start | bytes 294916
  469.9 46.7 %copy-start.42 = (f32[6,512]{1,0:T(8,128)S(1)}, f32[6,512]{1,0:T(8,128)}, u32[]{:S(2)}) copy-start(f32[6,512]{1,0:T(8,128)} %copy-done.41) | copy-start | bytes 36868
  470.0 47.6 %copy-start.28 = (f32[8,3072]{1,0:T(8,128)}, f32[8,3072]{1,0:T(8,128)S(1)}, u32[]{:S(2)}) copy-start(f32[8,3072]{1,0:T(8,128)S(1)} %multiply_subtract_fusion.2) | copy-start | bytes 294916
  473.3 45.6 %copy-start.35 = (s32[3072]{0:T(1024)S(1)}, s32[3072]{0:T(1024)}, u32[]{:S(2)}) copy-start(s32[3072]{0:T(1024)} %copy-done.34) | copy-start | bytes 36868
  529.8 43.8 %copy-start.4 = (f32[8,3072]{1,0:T(8,128)S(1)}, f32[8,3072]{1,0:T(8,128)}, u32[]{:S(2)}) copy-start(f32[8,3072]{1,0:T(8,128)} %copy-done.3) | copy-start | bytes 294916
  601.3 10.3 %collective-permute-start.24 = (f32[8,512]{1,0:T(8,128)S(1)}, f32[8,512]{1,0:T(8,128)S(1)}, u32[]{:S(2)}, u32[]{:S(2)}) collective-permute-start(f32[8,512]{1,0:T(8,128)S(1)} %get-tuple-element.175), channel_id=1, source_target_pairs={{0,1},{1,2},{2,3},{3,4},{4,5},{5,6},{6,7},{7,8},{8,9},{9,10},{10,1... | collective-permute-start | bytes 49160 | tf_op jit(solution)/shard_map/ppermute | solution.py:18
  601.6 13.6 %collective-permute-start.25 = (f32[8,512]{1,0:T(8,128)S(1)}, f32[8,512]{1,0:T(8,128)S(1)}, u32[]{:S(2)}, u32[]{:S(2)}) collective-permute-start(f32[8,512]{1,0:T(8,128)S(1)} %get-tuple-element.174), channel_id=1, source_target_pairs={{0,31},{1,0},{2,1},{3,2},{4,3},{5,4},{6,5},{7,6},{8,7},{9,8},{10,9... | collective-permute-start | bytes 49160 | tf_op jit(solution)/shard_map/ppermute | solution.py:18
  606.9 8.9 collective-permute-start.26
  606.9 9.5 collective-permute-start.27
  611.6 5.3 collective-permute-start.28
  611.6 6.0 collective-permute-start.29
  621.9 53.9 %copy-start.75 = (f32[8]{0:T(128)S(1)}, f32[8]{0:T(128)}, u32[]{:S(2)}) copy-start(f32[8]{0:T(128)} %copy-done.74) | copy-start | bytes 100
  621.9 53.9 %copy-start.30 = (f32[8,3072]{1,0:T(8,128)S(1)}, f32[8,3072]{1,0:T(8,128)}, u32[]{:S(2)}) copy-start(f32[8,3072]{1,0:T(8,128)} %copy-done.28) | copy-start | bytes 294916
  675.8 43.7 %copy-start.72 = (f32[8]{0:T(128)}, f32[8]{0:T(128)S(1)}, u32[]{:S(2)}) copy-start(f32[8]{0:T(128)S(1)} %div.51) | copy-start | bytes 100
  675.8 47.9 %copy-start.43 = (f32[6,512]{1,0:T(8,128)S(1)}, f32[6,512]{1,0:T(8,128)}, u32[]{:S(2)}) copy-start(f32[6,512]{1,0:T(8,128)} %copy-done.41) | copy-start | bytes 36868
  737.9 43.6 %copy-start.76 = (f32[8]{0:T(128)S(1)}, f32[8]{0:T(128)}, u32[]{:S(2)}) copy-start(f32[8]{0:T(128)} %copy-done.74) | copy-start | bytes 100
  809.7 10.1 %collective-permute-start.30 = (f32[8,512]{1,0:T(8,128)S(1)}, f32[8,512]{1,0:T(8,128)S(1)}, u32[]{:S(2)}, u32[]{:S(2)}) collective-permute-start(f32[8,512]{1,0:T(8,128)S(1)} %get-tuple-element.169), channel_id=1, source_target_pairs={{0,1},{1,2},{2,3},{3,4},{4,5},{5,6},{6,7},{7,8},{8,9},{9,10},{10,1... | collective-permute-start | bytes 49160 | tf_op jit(solution)/shard_map/ppermute | solution.py:18
  809.8 13.6 %collective-permute-start.31 = (f32[8,512]{1,0:T(8,128)S(1)}, f32[8,512]{1,0:T(8,128)S(1)}, u32[]{:S(2)}, u32[]{:S(2)}) collective-permute-start(f32[8,512]{1,0:T(8,128)S(1)} %get-tuple-element.168), channel_id=1, source_target_pairs={{0,31},{1,0},{2,1},{3,2},{4,3},{5,4},{6,5},{7,6},{8,7},{9,8},{10,9... | collective-permute-start | bytes 49160 | tf_op jit(solution)/shard_map/ppermute | solution.py:18
  815.1 8.9 collective-permute-start.32
  815.1 9.5 collective-permute-start.33
  819.8 5.3 collective-permute-start.34
  819.8 5.9 collective-permute-start.35
  830.1 54.1 %copy-start.78 = (f32[8]{0:T(128)S(1)}, f32[8]{0:T(128)}, u32[]{:S(2)}) copy-start(f32[8]{0:T(128)} %copy-done.77) | copy-start | bytes 100
  830.1 54.1 %copy-start.5 = (f32[8,3072]{1,0:T(8,128)S(1)}, f32[8,3072]{1,0:T(8,128)}, u32[]{:S(2)}) copy-start(f32[8,3072]{1,0:T(8,128)} %copy-done.3) | copy-start | bytes 294916
  830.2 54.1 %copy-start.40 = (f32[8,3072]{1,0:T(8,128)S(1)}, f32[8,3072]{1,0:T(8,128)}, u32[]{:S(2)}) copy-start(f32[8,3072]{1,0:T(8,128)} %copy-done.39) | copy-start | bytes 294916
  830.2 54.1 %copy-start.71 = (f32[8]{0:T(128)S(1)}, f32[8]{0:T(128)}, u32[]{:S(2)}) copy-start(f32[8]{0:T(128)} %copy-done.70) | copy-start | bytes 100
  830.2 54.1 %copy-start.73 = (f32[8]{0:T(128)S(1)}, f32[8]{0:T(128)}, u32[]{:S(2)}) copy-start(f32[8]{0:T(128)} %copy-done.72) | copy-start | bytes 100
  843.6 41.5 %copy-start.8 = (f32[8,3072]{1,0:T(8,128)S(1)}, f32[8,3072]{1,0:T(8,128)}, u32[]{:S(2)}) copy-start(f32[8,3072]{1,0:T(8,128)} %copy-done.6) | copy-start | bytes 294916
  884.3 47.3 %copy-start.44 = (f32[6,512]{1,0:T(8,128)S(1)}, f32[6,512]{1,0:T(8,128)}, u32[]{:S(2)}) copy-start(f32[6,512]{1,0:T(8,128)} %copy-done.41) | copy-start | bytes 36868
  888.3 44.1 %copy-start.36 = (s32[3072]{0:T(1024)S(1)}, s32[3072]{0:T(1024)}, u32[]{:S(2)}) copy-start(s32[3072]{0:T(1024)} %copy-done.34) | copy-start | bytes 36868
  (54 other events, 581.7 us)
